TPU v7x, 32 devices: a whole 2x2x4 slice. The times are simulated.
32 devices in a mesh: row: 4 (over y, core), col: 8 (over z, x).
Axes of the slice: x: 2, y: 2, z: 4, core: 2. Of those that a mesh axis runs over, the one named last changes fastest.
Arguments:
- queries: bfloat16 [128, 128, 1024], P(('row', 'col')), may hold values from -6 to 6
- coarse_keys: bfloat16 [512, 1024], P('row'), may hold values from -6 to 6
- fine_keys: bfloat16 [4096, 1024], P('col'), may hold values from -6 to 6
- super_ids: int32 [128, 16], P(('row', 'col')), may hold values from 0 to 511, as said below
- picks: int32 [128, 64], P(('row', 'col')), may hold values from 0 to 127, as said below
Outputs:
- importance: float32 [128, 8, 512], P(('row', 'col'))
- selected: float32 [128, 512], P(('row', 'col'))
Inputs may be any that keep to these rules, and one draw needn't show every extreme that they name: `super_ids`: within each aligned run of 4 query blocks (the query blocks of one device), at most 16 of the ids lie in any one aligned range of 64 superblocks, and some range holds exactly 16; in some aligned group of 8 consecutive runs, one range holds exactly 16 ids of every run. Ids may repeat. `picks`: the numbers of a row are distinct; pick p names fine block p % 8 of superblock super_ids[b, p // 8]. Within each aligned run of 4 query blocks, at most 64 of the named fine blocks lie in any one aligned range of 64 superblocks, and some range holds exactly 64.
All inputs are finite; a program needn't handle non-finite values.
Results may differ from a plain program's by a relative error of at most 0.0003.
Values may be sent and summed in bfloat16 or wider, within the bound.
A program may use at most 64 MiB of HBM per device.

v0:
```python
import math
import jax
import jax.numpy as jnp
from jax import lax
from jax.sharding import PartitionSpec as P

H = 8
D = 128
SBLK = 8
PICK = 64


def pack_requests(owners, local_ids, ncols, capacity):
    marks = (owners[:, None] == jnp.arange(ncols, dtype=jnp.int32)[None, :]).astype(jnp.int32)
    earlier = jnp.cumsum(marks, axis=0) - marks
    slots = jnp.sum(earlier * marks, axis=1)
    places = owners * capacity + slots
    cells = jnp.arange(ncols * capacity, dtype=jnp.int32)
    matches = places[:, None] == cells[None, :]
    outgoing = jnp.sum(jnp.where(matches, local_ids[:, None] + 1, 0), axis=0) - 1
    return (outgoing.reshape(ncols, capacity), places)


def per_device(queries, coarse_keys, fine_keys, super_ids, picks):
    factor = 1.0 / math.sqrt(D)
    blocks, qtok, width = queries.shape
    supers = coarse_keys.shape[0] * lax.axis_size("row")
    ncols = lax.axis_size("col")
    qheads = queries.reshape(blocks, qtok, H, D)

    def block_scores(query_block, block_keys):
        keyed = block_keys.reshape(block_keys.shape[0], H, D)
        return (
            jnp.einsum("thd,nhd->htn", query_block, keyed, preferred_element_type=jnp.float32)
            * factor
        )

    start_max = jnp.full((blocks, H, qtok), -1e30, jnp.float32)
    start_totals = jnp.zeros((blocks, H, qtok), jnp.float32)
    gathered = lax.all_gather(coarse_keys, "row", axis=0, tiled=True)

    def stat_per_block(inputs):
        query_block, running_max, totals = inputs
        scores = block_scores(query_block, gathered)
        new_max = jnp.maximum(running_max, jnp.max(scores, axis=-1))
        totals = totals * jnp.exp(running_max - new_max) + jnp.sum(
            jnp.exp(scores - new_max[..., None]), axis=-1
        )
        return (new_max, totals)

    running_max, totals = lax.map(stat_per_block, (qheads, start_max, start_totals))

    def make_per_block(inputs):
        query_block, block_max, block_totals = inputs
        scores = block_scores(query_block, gathered)
        softened = jnp.exp(scores - block_max[..., None]) / block_totals[..., None]
        return jnp.sum(softened, axis=1) * (supers / qtok)

    portion = lax.map(make_per_block, (qheads, running_max, totals))
    sup_dev = fine_keys.shape[0] // SBLK
    parents = jnp.take_along_axis(super_ids, picks // SBLK, axis=1)
    capacity = blocks // 4 * PICK
    span = sup_dev * SBLK
    fine_ids = parents * SBLK + picks % SBLK
    owners = (fine_ids // span).reshape(-1)
    local_ids = (fine_ids % span).reshape(-1)
    outgoing, places = pack_requests(owners, local_ids, ncols, capacity)
    found = jnp.take(
        fine_keys,
        jnp.clip(
            lax.all_to_all(outgoing, "col", split_axis=0, concat_axis=0, tiled=True), 0, span - 1
        ),
        axis=0,
    )
    replies = lax.all_to_all(found, "col", split_axis=0, concat_axis=0, tiled=True)
    fetched = jnp.take(replies.reshape(ncols * capacity, width), places, axis=0)
    fetched = fetched.reshape(blocks, PICK, H, D)
    weights = jnp.take_along_axis(
        portion, jnp.broadcast_to(parents[:, None, :], (blocks, H, PICK)), axis=2
    )
    scores = (
        jnp.einsum("bthd,bjhd->bhtj", qheads, fetched, preferred_element_type=jnp.float32) * factor
    )
    softened = jax.nn.softmax(scores, axis=-1)
    selected = jnp.sum(softened, axis=2) * weights * (PICK / qtok)
    return (portion, selected.reshape(blocks, H * PICK))


def solution(mesh):
    return jax.shard_map(
        per_device,
        mesh=mesh,
        in_specs=(
            P(("row", "col"), None, None),
            P("row", None),
            P("col", None),
            P(("row", "col"), None),
            P(("row", "col"), None),
        ),
        out_specs=(P(("row", "col"), None, None), P(("row", "col"), None)),
        check_vma=False,
    )
```

profile of v0, /device:TPU:0, one launch (start us, length us, event | category | flops | bytes accessed | tf_op | source)
XLA Modules:
  0.0 85.9 jit_solution(12894194768072370491)
XLA Ops:
  7.2 0.0 copy-start
  7.2 0.0 copy-start.5
  7.2 0.0 copy-start.4
  7.2 0.8 bitcast_or_fusion
  8.0 0.1 reshape.247
  8.1 2.3 %gather_fusion.2 = s32[256]{0:T(256)S(1)} fusion(s32[4,16]{1,0:T(4,128)} %param.12, s32[256]{0:T(256)S(1)} %reshape.247), kind=kCustom, calls=%fused_computation.2 | custom fusion | bytes 4096 | tf_op jit(solution)/shard_map/jit(take_along_axis)/gather | solution.py:61
  10.5 0.1 reshape.250
  10.5 0.0 copy-done.5
  10.6 0.1 eq.42
  10.7 0.1 reshape.225
  10.8 0.6 reduce-window.6
  11.3 0.2 slice_reduce_fusion
  11.6 0.1 fusion.25
  11.7 0.1 add.141
  11.8 0.1 select_reduce_fusion
  11.9 0.7 sub.59
  12.6 7.3 %all-to-all-start = ((s32[8,1,64]{2,1,0:T(1,128)}), s32[8,1,64]{2,1,0:T(1,128)S(1)}, u32[]{:S(2)}, u32[]{:S(2)}) async-start(s32[8,1,64]{2,1,0:T(1,128)} %sub.59), calls=%async_computation | async-start | bytes 8192 | tf_op jit(solution)/shard_map/all_to_all | solution.py:71
  19.9 0.0 all-gather.2.cloned.1.call-start
  19.9 0.7 all-gather.2.cloned.1.call-update
  20.6 0.1 reduce_sum.63
  20.7 0.1 mul.88
  20.9 0.0 copy-done.4
  20.9 0.7 copy.26
  21.6 0.0 copy-start.2
  21.6 1.0 %copy-done.2 = bf16[4,128,1024]{1,2,0:T(8,128)(2,1)} copy-done((bf16[4,128,1024]{1,2,0:T(8,128)(2,1)}, bf16[4,128,1024]{1,2,0:T(8,128)(2,1)S(1)}, u32[]{:S(2)}) %copy-start.2) | copy-done | bytes 1048600
  22.5 0.7 copy.28
  23.2 0.1 reshape.253
  23.3 3.0 %all-to-all-done = s32[8,1,64]{2,1,0:T(1,128)S(1)} async-done(((s32[8,1,64]{2,1,0:T(1,128)}), s32[8,1,64]{2,1,0:T(1,128)S(1)}, u32[]{:S(2)}, u32[]{:S(2)}) %all-to-all-start) | async-done | bytes 2080 | tf_op jit(solution)/shard_map/all_to_all | solution.py:71
  26.3 0.1 reshape.233
  26.4 0.0 copy-done
  26.4 2.1 %gather_fusion = bf16[512,1024]{1,0:T(8,128)(2,1)S(1)} fusion(bf16[512,1024]{1,0:T(8,128)(2,1)S(1)} %copy-done, s32[1024]{0:T(1024)S(1)} %pad_clamp_fusion.1), kind=kCustom, calls=%fused_computation | custom fusion | bytes 2099200 | tf_op jit(solution)/shard_map/jit(_take)/gather | solution.py:68
  28.5 1.2 %broadcast_select_fusion = bf16[8,64,1024]{2,1,0:T(8,128)(2,1)} fusion(bf16[8,64,1024]{2,1,0:T(8,128)(2,1)S(1)} %bitcast.99, pred[8,64]{1,0:T(8,128)(4,1)S(1)} %compare_and_fusion), kind=kLoop, calls=%fused_computation.36 | loop fusion | flops 524288 | bytes 2097664 | tf_op jit(solution)/shard_map/jit(_take)/select_n | solution.py:68
  29.7 3.6 %all-to-all-start.1 = ((bf16[8,64,1024]{2,1,0:T(8,128)(2,1)}), bf16[8,64,1024]{2,1,0:T(8,128)(2,1)S(1)}, u32[]{:S(2)}, u32[]{:S(2)}) async-start(bf16[8,64,1024]{2,1,0:T(8,128)(2,1)} %broadcast_select_fusion), calls=%async_computation.1 | async-start | bytes 2097152 | tf_op jit(solution)/shard_map/all_to_all | solution.py:75
  33.2 7.2 %all-gather.2.cloned.1.call-done = bf16[512,1024]{1,0:T(8,128)(2,1)} async-done(((bf16[128,1024]{1,0:T(8,128)(2,1)}), bf16[512,1024]{1,0:T(8,128)(2,1)}) %all-gather.2.cloned.1.call-update) | async-done | bytes 1048592 | tf_op jit(solution)/shard_map/all_gather | solution.py:40
  40.4 9.6 %while.22 = (s32[]{:T(128)}, f32[4,8,128]{2,1,0:T(8,128)S(1)}, f32[4,8,128]{2,1,0:T(8,128)S(1)}, bf16[4,128,8,128]{3,1,2,0:T(8,128)(2,1)S(1)}, bf16[512,1024]{1,0:T(8,128)(2,1)}, /*index=5*/s32[]{:T(128)}) while((s32[]{:T(128)}, f32[4,8,128]{2,1,0:T(8,128)S(1)}, f32[4,8,128]{2,1,0:T(8,128)S(1)}, bf16[4,128,8,128]{3,1,2,0:T(8,128)(2,1)S(1)}, ...), condition=%wide.region_3.4_spmd, body=%wide.region_0.3_spmd.sunk | while | flops 136842240 | bytes 5541965 | solution.py:51
  40.4 1.8 %multiply_reduce_fusion.2 = (f32[8,128]{1,0:T(8,128)S(1)}, f32[8,128,512]{2,1,0:T(8,128)S(1)}) fusion(bf16[4,128,8,128]{3,1,2,0:T(8,128)(2,1)S(1)} %get-tuple-element.227, s32[]{:T(128)} %get-tuple-element.218, bf16[512,1024]{1,0:T(8,128)(2,1)} %get-tuple-element.228), kind=kOutput, calls=%fused_computation.5.clone.1 | convolution fusion | flops 135265280 | bytes 3411972 | tf_op jit(solution)/shard_map/while/body/eval_jaxpr/thd,nhd->htn/dot_general | solution.py:34
  42.2 0.6 exponential_reduce_fusion.2
  42.8 1.8 %multiply_reduce_fusion.2 = (f32[8,128]{1,0:T(8,128)S(1)}, f32[8,128,512]{2,1,0:T(8,128)S(1)}) fusion(bf16[4,128,8,128]{3,1,2,0:T(8,128)(2,1)S(1)} %get-tuple-element.227, s32[]{:T(128)} %get-tuple-element.218, bf16[512,1024]{1,0:T(8,128)(2,1)} %get-tuple-element.228), kind=kOutput, calls=%fused_computation.5.clone.1 | convolution fusion | flops 135265280 | bytes 3411972 | tf_op jit(solution)/shard_map/while/body/eval_jaxpr/thd,nhd->htn/dot_general | solution.py:34
  44.6 0.6 exponential_reduce_fusion.2
  45.2 1.8 %multiply_reduce_fusion.2 = (f32[8,128]{1,0:T(8,128)S(1)}, f32[8,128,512]{2,1,0:T(8,128)S(1)}) fusion(bf16[4,128,8,128]{3,1,2,0:T(8,128)(2,1)S(1)} %get-tuple-element.227, s32[]{:T(128)} %get-tuple-element.218, bf16[512,1024]{1,0:T(8,128)(2,1)} %get-tuple-element.228), kind=kOutput, calls=%fused_computation.5.clone.1 | convolution fusion | flops 135265280 | bytes 3411972 | tf_op jit(solution)/shard_map/while/body/eval_jaxpr/thd,nhd->htn/dot_general | solution.py:34
  47.0 0.6 exponential_reduce_fusion.2
  47.6 1.8 %multiply_reduce_fusion.2 = (f32[8,128]{1,0:T(8,128)S(1)}, f32[8,128,512]{2,1,0:T(8,128)S(1)}) fusion(bf16[4,128,8,128]{3,1,2,0:T(8,128)(2,1)S(1)} %get-tuple-element.227, s32[]{:T(128)} %get-tuple-element.218, bf16[512,1024]{1,0:T(8,128)(2,1)} %get-tuple-element.228), kind=kOutput, calls=%fused_computation.5.clone.1 | convolution fusion | flops 135265280 | bytes 3411972 | tf_op jit(solution)/shard_map/while/body/eval_jaxpr/thd,nhd->htn/dot_general | solution.py:34
  49.4 0.6 exponential_reduce_fusion.2
  50.0 8.1 %while.23 = (s32[]{:T(128)}, f32[4,8,512]{2,1,0:T(8,128)S(1)}, bf16[4,128,8,128]{3,1,2,0:T(8,128)(2,1)S(1)}, bf16[512,1024]{1,0:T(8,128)(2,1)}, f32[4,8,128]{2,1...) while((s32[]{:T(128)}, f32[4,8,512]{2,1,0:T(8,128)S(1)}, bf16[4,128,8,128]{3,1,2,0:T(8,128)(2,1)S(1)}, ...), condition=%wide.region_6.7_spmd, body=%wide.region_4.6_spmd.sunk | while | flops 136314880 | bytes 1384537 | solution.py:59
  50.0 2.0 %fusion.49 = f32[8,512]{1,0:T(8,128)S(1)} fusion(f32[8,128]{1,0:T(8,128)S(1)} %get-tuple-element.210, f32[8,128]{1,0:T(8,128)S(1)} %get-tuple-element.211, bf16[4,128,8,128]{3,1,2,0:T(8,128)(2,1)S(1)} %get-tuple-element.246, s32[]{:T(128)} %get-tuple-element.237, bf16[512,1024]{1,0:T(8,128)(2,1)} %get-tuple-element.247), kind=kOutput, calls=%fused_computation.20.clone.1 | convolution fusion | flops 136310784 | bytes 1335300 | tf_op jit(solution)/shard_map/while/body/eval_jaxpr/thd,nhd->htn/dot_general | solution.py:34
  52.1 2.0 %fusion.49 = f32[8,512]{1,0:T(8,128)S(1)} fusion(f32[8,128]{1,0:T(8,128)S(1)} %get-tuple-element.210, f32[8,128]{1,0:T(8,128)S(1)} %get-tuple-element.211, bf16[4,128,8,128]{3,1,2,0:T(8,128)(2,1)S(1)} %get-tuple-element.246, s32[]{:T(128)} %get-tuple-element.237, bf16[512,1024]{1,0:T(8,128)(2,1)} %get-tuple-element.247), kind=kOutput, calls=%fused_computation.20.clone.1 | convolution fusion | flops 136310784 | bytes 1335300 | tf_op jit(solution)/shard_map/while/body/eval_jaxpr/thd,nhd->htn/dot_general | solution.py:34
  54.1 2.0 %fusion.49 = f32[8,512]{1,0:T(8,128)S(1)} fusion(f32[8,128]{1,0:T(8,128)S(1)} %get-tuple-element.210, f32[8,128]{1,0:T(8,128)S(1)} %get-tuple-element.211, bf16[4,128,8,128]{3,1,2,0:T(8,128)(2,1)S(1)} %get-tuple-element.246, s32[]{:T(128)} %get-tuple-element.237, bf16[512,1024]{1,0:T(8,128)(2,1)} %get-tuple-element.247), kind=kOutput, calls=%fused_computation.20.clone.1 | convolution fusion | flops 136310784 | bytes 1335300 | tf_op jit(solution)/shard_map/while/body/eval_jaxpr/thd,nhd->htn/dot_general | solution.py:34
  56.1 2.0 %fusion.49 = f32[8,512]{1,0:T(8,128)S(1)} fusion(f32[8,128]{1,0:T(8,128)S(1)} %get-tuple-element.210, f32[8,128]{1,0:T(8,128)S(1)} %get-tuple-element.211, bf16[4,128,8,128]{3,1,2,0:T(8,128)(2,1)S(1)} %get-tuple-element.246, s32[]{:T(128)} %get-tuple-element.237, bf16[512,1024]{1,0:T(8,128)(2,1)} %get-tuple-element.247), kind=kOutput, calls=%fused_computation.20.clone.1 | convolution fusion | flops 136310784 | bytes 1335300 | tf_op jit(solution)/shard_map/while/body/eval_jaxpr/thd,nhd->htn/dot_general | solution.py:34
  58.1 0.0 copy-start.1
  58.1 16.3 %gather_fusion.3 = f32[2048]{0:T(1024)S(1)} fusion(f32[4,8,512]{2,1,0:T(8,128)S(1)} %get-tuple-element.60, s32[2048]{0:T(1024)S(1)} %reshape.253), kind=kCustom, calls=%fused_computation.3 | custom fusion | bytes 40960 | tf_op jit(solution)/shard_map/jit(take_along_axis)/gather | solution.py:78
  74.4 0.0 copy-done.1
  74.4 0.1 reshape.256
  74.5 0.0 all-to-all-done.1
  74.5 0.0 copy-start.3
  74.5 2.0 %gather_fusion.1 = bf16[256,1024]{1,0:T(8,128)(2,1)} fusion(bf16[512,1024]{1,0:T(8,128)(2,1)S(1)} %bitcast.98, s32[1024]{0:T(1024)S(1)} %pad_clamp_fusion), kind=kCustom, calls=%fused_computation.1 | custom fusion | bytes 1049600 | tf_op jit(solution)/shard_map/jit(_take)/gather | solution.py:76
  76.5 1.1 %copy.34 = bf16[32,8,8,128]{3,2,1,0:T(8,128)(2,1)S(1)} copy(bf16[32,8,8,128]{3,1,2,0:T(8,128)(2,1)} %bitcast.102) | data formatting | bytes 1048576
  77.6 0.0 copy-done.3
  77.6 0.7 fusion.34
  78.3 0.7 reshape.230
  (36 shorter events, 0.3 us)
Async XLA Ops:
  7.2 19.3 %copy-start = (bf16[512,1024]{1,0:T(8,128)(2,1)S(1)}, bf16[512,1024]{1,0:T(8,128)(2,1)}, u32[]{:S(2)}) copy-start(bf16[512,1024]{1,0:T(8,128)(2,1)} %param.11) | copy-start | bytes 3145732
  7.2 3.4 %copy-start.5 = (s32[4,64]{1,0:T(4,128)S(1)}, s32[4,64]{1,0:T(4,128)}, u32[]{:S(2)}) copy-start(s32[4,64]{1,0:T(4,128)} %param.13) | copy-start | bytes 3076
  7.2 13.7 %copy-start.4 = (bf16[4,128,1024]{2,1,0:T(8,128)(2,1)S(1)}, bf16[4,128,1024]{2,1,0:T(8,128)(2,1)}, u32[]{:S(2)}) copy-start(bf16[4,128,1024]{2,1,0:T(8,128)(2,1)} %param.9) | copy-start | bytes 3145732
  12.6 13.7 %all-to-all-start = ((s32[8,1,64]{2,1,0:T(1,128)}), s32[8,1,64]{2,1,0:T(1,128)S(1)}, u32[]{:S(2)}, u32[]{:S(2)}) async-start(s32[8,1,64]{2,1,0:T(1,128)} %sub.59), calls=%async_computation | async-start | bytes 8192 | tf_op jit(solution)/shard_map/all_to_all | solution.py:71
  19.9 20.5 %all-gather.2.cloned.1.call-start = ((), (), s32[]{:S(2)}) async-start(), calls=%async_computation.2 | async-start | bytes 1310720 | tf_op jit(solution)/shard_map/all_gather | solution.py:40
  21.6 1.0 %copy-start.2 = (bf16[4,128,1024]{1,2,0:T(8,128)(2,1)}, bf16[4,128,1024]{1,2,0:T(8,128)(2,1)S(1)}, u32[]{:S(2)}) copy-start(bf16[4,128,1024]{1,2,0:T(8,128)(2,1)S(1)} %copy.26) | copy-start | bytes 3145732
  29.7 44.8 %all-to-all-start.1 = ((bf16[8,64,1024]{2,1,0:T(8,128)(2,1)}), bf16[8,64,1024]{2,1,0:T(8,128)(2,1)S(1)}, u32[]{:S(2)}, u32[]{:S(2)}) async-start(bf16[8,64,1024]{2,1,0:T(8,128)(2,1)} %broadcast_select_fusion), calls=%async_computation.1 | async-start | bytes 2097152 | tf_op jit(solution)/shard_map/all_to_all | solution.py:75
  58.1 16.3 %copy-start.1 = (f32[4,8,512]{2,1,0:T(8,128)}, f32[4,8,512]{2,1,0:T(8,128)S(1)}, u32[]{:S(2)}) copy-start(f32[4,8,512]{2,1,0:T(8,128)S(1)} %get-tuple-element.60) | copy-start | bytes 196612
  74.5 3.1 %copy-start.3 = (bf16[4,128,1024]{1,2,0:T(8,128)(2,1)S(1)}, bf16[4,128,1024]{1,2,0:T(8,128)(2,1)}, u32[]{:S(2)}) copy-start(bf16[4,128,1024]{1,2,0:T(8,128)(2,1)} %copy-done.2) | copy-start | bytes 3145732
Sparse Core Ops, SparseCore 0:
  22.3 18.1 all-gather.1
where the time goes:
time: 86.5 us; the launch traced here: 85.9 us
  local copies, waits for them, and re-layouts  28.5 us (33%)
  matrix products  15.6 us (18%)
  between operations  14.3 us (17%)
  starting transfers between devices  10.9 us (13%)
  waiting for transfers between devices  10.9 us (13%)
  other arithmetic  5.45 us (6%)
    gather x3, local copies, waits for them, and re-layouts, per_device(): jnp.take_along_axis(portion, jnp.broadcast_to(parents[:, None, :], (block...  16.4 us
    dot_general x8, matrix products, block_scores(): jnp.einsum('thd,nhd->htn', query_block, keyed, preferred_element_type=jnp...  14.9 us
    all_to_all x1, starting transfers between devices, per_device(): lax.all_to_all(outgoing, 'col', split_axis=0, concat_axis=0, tiled=True)  7.28 us
    all_gather x1, waiting for transfers between devices, per_device(): gathered = lax.all_gather(coarse_keys, 'row', axis=0, tiled=True)  7.22 us
    all_to_all x1, starting transfers between devices, per_device(): lax.all_to_all(found, 'col', split_axis=0, concat_axis=0, tiled=True)  3.56 us
    all_to_all x1, waiting for transfers between devices, per_device(): lax.all_to_all(outgoing, 'col', split_axis=0, concat_axis=0, tiled=True)  3.04 us
    unnamed x14, local copies, waits for them, and re-layouts  2.8 us
    gather x3, local copies, waits for them, and re-layouts, per_device(): parents = jnp.take_along_axis(super_ids, picks // SBLK, axis=1)  2.49 us
  transfers between devices with their start and end apart: 3, of which 2 were waited for; matrix products, arithmetic and copies ran while one was open for 45% of the time, Pallas kernels for 0%

commit v1 on v0

--- a/solution.py
+++ b/solution.py
@@ -37,7 +37,12 @@
 
     start_max = jnp.full((blocks, H, qtok), -1e30, jnp.float32)
     start_totals = jnp.zeros((blocks, H, qtok), jnp.float32)
-    gathered = lax.all_gather(coarse_keys, "row", axis=0, tiled=True)
+    ring = [coarse_keys]
+    for hop in range(3):
+        ring.append(lax.ppermute(ring[-1], "row", [(dev, (dev + 1) % 4) for dev in range(4)]))
+    gathered = jnp.roll(
+        jnp.concatenate(ring[::-1], axis=0), (lax.axis_index("row") + 1) * ring[0].shape[0], axis=0
+    )
 
     def stat_per_block(inputs):
         query_block, running_max, totals = inputs

time: 86.5 us -> 69.1 us (0.80)
  between operations: 14.3 us -> 0.96 us
  waiting for transfers between devices: 10.9 us -> 7.64 us
  matrix products: 15.6 us -> 13.4 us
  local copies, waits for them, and re-layouts: 28.5 us -> 29.4 us
    all_gather x1 -> x0, waiting for transfers between devices: 7.22 us -> none  [per_device(): gathered = lax.all_gather(coarse_keys, 'row', axis=0, tiled=True)]
    ppermute x0 -> x3, waiting for transfers between devices: none -> 4.55 us  [per_device(): lax.ppermute(ring[-1], 'row', [(dev, (dev + 1) % 4) for dev in range(4)])]
    dot_general x8, matrix products: 14.9 us -> 12.7 us  [block_scores(): jnp.einsum('thd,nhd->htn', query_block, keyed, preferred_element_type=jnp...]
    unnamed x14 -> x23, local copies, waits for them, and re-layouts: 2.8 us -> 2.94 us
  transfers between devices with their start and end apart: 3 -> 5, of which waited for: 2 -> 3; matrix products, arithmetic and copies ran while one was open for 45% -> 62% of each run, Pallas kernels for 0% -> 0%
where the time goes in v1:
time: 69.1 us; the launch traced here: 68.3 us
  local copies, waits for them, and re-layouts  29.4 us (43%)
  matrix products  13.4 us (19%)
  starting transfers between devices  11.2 us (16%)
  waiting for transfers between devices  7.64 us (11%)
  other arithmetic  5.35 us (8%)
  between operations  0.96 us (1%)
    gather x3, local copies, waits for them, and re-layouts, per_device(): jnp.take_along_axis(portion, jnp.broadcast_to(parents[:, None, :], (block...  16.4 us
    dot_general x8, matrix products, block_scores(): jnp.einsum('thd,nhd->htn', query_block, keyed, preferred_element_type=jnp...  12.7 us
    all_to_all x1, starting transfers between devices, per_device(): lax.all_to_all(outgoing, 'col', split_axis=0, concat_axis=0, tiled=True)  6.94 us
    ppermute x3, waiting for transfers between devices, per_device(): lax.ppermute(ring[-1], 'row', [(dev, (dev + 1) % 4) for dev in range(4)])  4.55 us
    all_to_all x1, starting transfers between devices, per_device(): lax.all_to_all(found, 'col', split_axis=0, concat_axis=0, tiled=True)  3.69 us
    all_to_all x1, waiting for transfers between devices, per_device(): lax.all_to_all(outgoing, 'col', split_axis=0, concat_axis=0, tiled=True)  3.09 us
    unnamed x23, local copies, waits for them, and re-layouts  2.94 us
    gather x3, local copies, waits for them, and re-layouts, per_device(): parents = jnp.take_along_axis(super_ids, picks // SBLK, axis=1)  2.49 us
  transfers between devices with their start and end apart: 5, of which 3 were waited for; matrix products, arithmetic and copies ran while one was open for 62% of the time, Pallas kernels for 0%

profile of v1, /device:TPU:0, one launch (start us, length us, event | category | flops | bytes accessed | tf_op | source)
XLA Modules:
  0.0 68.3 jit_solution(7427949627741404073)
XLA Ops:
  0.6 0.0 copy-start
  0.6 0.0 copy-start.6
  0.7 0.0 copy-start.4
  0.7 0.5 collective-permute-start
  1.2 0.7 %bitcast_or_fusion = s32[4,64,1]{1,0,2:T(4,128)S(1)} fusion(s32[4,64]{1,0:T(4,128)} %param.13), kind=kLoop, calls=%fused_computation.82 | loop fusion | flops 5888 | bytes 2048 | tf_op jit(solution)/shard_map/jit(take_along_axis)/gather | solution.py:66
  1.9 0.1 reshape.247
  2.0 2.3 %gather_fusion.2 = s32[256]{0:T(256)S(1)} fusion(s32[4,16]{1,0:T(4,128)} %param.12, s32[256]{0:T(256)S(1)} %reshape.247), kind=kCustom, calls=%fused_computation.2 | custom fusion | bytes 4096 | tf_op jit(solution)/shard_map/jit(take_along_axis)/gather | solution.py:66
  4.3 0.1 reshape.250
  4.4 0.0 copy-done.6
  4.4 0.1 eq.45
  4.5 0.1 reshape.225
  4.6 0.6 reduce-window.6
  5.2 0.2 slice_reduce_fusion
  5.4 0.1 fusion.25
  5.6 0.1 add.157
  5.6 0.1 select_reduce_fusion
  5.8 0.7 sub.64
  6.5 6.9 %all-to-all-start = ((s32[8,1,64]{2,1,0:T(1,128)}), s32[8,1,64]{2,1,0:T(1,128)S(1)}, u32[]{:S(2)}, u32[]{:S(2)}) async-start(s32[8,1,64]{2,1,0:T(1,128)} %sub.64), calls=%async_computation | async-start | bytes 8192 | tf_op jit(solution)/shard_map/all_to_all | solution.py:76
  13.4 0.1 reduce_sum.63
  13.5 0.1 mul.92
  13.7 0.0 copy-done.4
  13.7 0.7 copy.26
  14.4 0.0 copy-start.2
  14.4 1.0 %copy-done.2 = bf16[4,128,1024]{1,2,0:T(8,128)(2,1)} copy-done((bf16[4,128,1024]{1,2,0:T(8,128)(2,1)}, bf16[4,128,1024]{1,2,0:T(8,128)(2,1)S(1)}, u32[]{:S(2)}) %copy-start.2) | copy-done | bytes 1048600
  15.4 1.3 %copy.28 = bf16[4,128,8,128]{3,1,2,0:T(8,128)(2,1)} copy(bf16[4,128,8,128]{1,3,2,0:T(8,128)(2,1)S(1)} %bitcast.100) | data formatting | bytes 2097152 | tf_op jit(solution)/shard_map/while | solution.py:64
  16.7 0.1 reshape.253
  16.8 3.1 %all-to-all-done = s32[8,1,64]{2,1,0:T(1,128)S(1)} async-done(((s32[8,1,64]{2,1,0:T(1,128)}), s32[8,1,64]{2,1,0:T(1,128)S(1)}, u32[]{:S(2)}, u32[]{:S(2)}) %all-to-all-start) | async-done | bytes 2080 | tf_op jit(solution)/shard_map/all_to_all | solution.py:76
  19.9 0.1 reshape.233
  19.9 0.0 collective-permute-done
  19.9 0.1 collective-permute-start.1
  20.0 0.0 copy-done
  20.0 2.1 %gather_fusion = bf16[512,1024]{1,0:T(8,128)(2,1)S(1)} fusion(bf16[512,1024]{1,0:T(8,128)(2,1)S(1)} %copy-done, s32[1024]{0:T(1024)S(1)} %pad_clamp_fusion.1), kind=kCustom, calls=%fused_computation | custom fusion | bytes 2099200 | tf_op jit(solution)/shard_map/jit(_take)/gather | solution.py:73
  22.1 3.6 %collective-permute-done.1 = bf16[128,1024]{1,0:T(8,128)(2,1)S(1)} collective-permute-done((bf16[128,1024]{1,0:T(8,128)(2,1)S(1)}, bf16[128,1024]{1,0:T(8,128)(2,1)S(1)}, u32[]{:S(2)}, u32[]{:S(2)}) %collective-permute-start.1) | collective-permute-done | bytes 262176 | tf_op jit(solution)/shard_map/ppermute | solution.py:42
  25.7 0.0 collective-permute-start.2
  25.7 1.2 %broadcast_select_fusion = bf16[8,64,1024]{2,1,0:T(8,128)(2,1)} fusion(bf16[8,64,1024]{2,1,0:T(8,128)(2,1)S(1)} %bitcast.99, pred[8,64]{1,0:T(8,128)(4,1)S(1)} %compare_and_fusion), kind=kLoop, calls=%fused_computation.36 | loop fusion | flops 524288 | bytes 2097664 | tf_op jit(solution)/shard_map/jit(_take)/select_n | solution.py:73
  26.9 3.7 %all-to-all-start.1 = ((bf16[8,64,1024]{2,1,0:T(8,128)(2,1)}), bf16[8,64,1024]{2,1,0:T(8,128)(2,1)S(1)}, u32[]{:S(2)}, u32[]{:S(2)}) async-start(bf16[8,64,1024]{2,1,0:T(8,128)(2,1)} %broadcast_select_fusion), calls=%async_computation.1 | async-start | bytes 2097152 | tf_op jit(solution)/shard_map/all_to_all | solution.py:80
  30.6 0.9 %collective-permute-done.2 = bf16[128,1024]{1,0:T(8,128)(2,1)S(1)} collective-permute-done((bf16[128,1024]{1,0:T(8,128)(2,1)S(1)}, bf16[128,1024]{1,0:T(8,128)(2,1)S(1)}, u32[]{:S(2)}, u32[]{:S(2)}) %collective-permute-start.2) | collective-permute-done | bytes 262176 | tf_op jit(solution)/shard_map/ppermute | solution.py:42
  31.6 0.0 copy-done.5
  31.8 0.1 constant_dynamic-slice_fusion
  31.8 8.5 %while.22 = (s32[]{:T(128)}, f32[4,8,128]{2,1,0:T(8,128)S(1)}, f32[4,8,128]{2,1,0:T(8,128)S(1)}, bf16[4,128,8,128]{3,1,2,0:T(8,128)(2,1)}, bf16[512,1024]{1,0:T(8,128)(2,1)S(1)}, /*index=5*/s32[]{:T(128)}) while((s32[]{:T(128)}, f32[4,8,128]{2,1,0:T(8,128)S(1)}, f32[4,8,128]{2,1,0:T(8,128)S(1)}, bf16[4,128,8,128]{3,1,2,0:T(8,128)(2,1)}, ...), condition=%wide.region_3.4_spmd, body=%wide.region_0.3_spmd.sunk | while | flops 136842240 | bytes 5542473 | solution.py:56
  31.9 1.5 %multiply_reduce_fusion.2 = (f32[8,128]{1,0:T(8,128)S(1)}, f32[8,128,512]{2,1,0:T(8,128)S(1)}) fusion(bf16[4,128,8,128]{3,1,2,0:T(8,128)(2,1)} %get-tuple-element.227, s32[]{:T(128)} %get-tuple-element.218, bf16[512,1024]{1,0:T(8,128)(2,1)S(1)} %get-tuple-element.228), kind=kOutput, calls=%fused_computation.5.clone.1 | convolution fusion | flops 135265280 | bytes 3412480 | tf_op jit(solution)/shard_map/while/body/eval_jaxpr/thd,nhd->htn/dot_general | solution.py:34
  33.3 0.6 exponential_reduce_fusion.2
  34.0 1.5 %multiply_reduce_fusion.2 = (f32[8,128]{1,0:T(8,128)S(1)}, f32[8,128,512]{2,1,0:T(8,128)S(1)}) fusion(bf16[4,128,8,128]{3,1,2,0:T(8,128)(2,1)} %get-tuple-element.227, s32[]{:T(128)} %get-tuple-element.218, bf16[512,1024]{1,0:T(8,128)(2,1)S(1)} %get-tuple-element.228), kind=kOutput, calls=%fused_computation.5.clone.1 | convolution fusion | flops 135265280 | bytes 3412480 | tf_op jit(solution)/shard_map/while/body/eval_jaxpr/thd,nhd->htn/dot_general | solution.py:34
  35.5 0.6 exponential_reduce_fusion.2
  36.1 1.5 %multiply_reduce_fusion.2 = (f32[8,128]{1,0:T(8,128)S(1)}, f32[8,128,512]{2,1,0:T(8,128)S(1)}) fusion(bf16[4,128,8,128]{3,1,2,0:T(8,128)(2,1)} %get-tuple-element.227, s32[]{:T(128)} %get-tuple-element.218, bf16[512,1024]{1,0:T(8,128)(2,1)S(1)} %get-tuple-element.228), kind=kOutput, calls=%fused_computation.5.clone.1 | convolution fusion | flops 135265280 | bytes 3412480 | tf_op jit(solution)/shard_map/while/body/eval_jaxpr/thd,nhd->htn/dot_general | solution.py:34
  37.6 0.6 exponential_reduce_fusion.2
  38.2 1.5 %multiply_reduce_fusion.2 = (f32[8,128]{1,0:T(8,128)S(1)}, f32[8,128,512]{2,1,0:T(8,128)S(1)}) fusion(bf16[4,128,8,128]{3,1,2,0:T(8,128)(2,1)} %get-tuple-element.227, s32[]{:T(128)} %get-tuple-element.218, bf16[512,1024]{1,0:T(8,128)(2,1)S(1)} %get-tuple-element.228), kind=kOutput, calls=%fused_computation.5.clone.1 | convolution fusion | flops 135265280 | bytes 3412480 | tf_op jit(solution)/shard_map/while/body/eval_jaxpr/thd,nhd->htn/dot_general | solution.py:34
  39.7 0.6 exponential_reduce_fusion.2
  40.3 7.0 %while.23 = (s32[]{:T(128)}, f32[4,8,512]{2,1,0:T(8,128)S(1)}, bf16[4,128,8,128]{3,1,2,0:T(8,128)(2,1)}, bf16[512,1024]{1,0:T(8,128)(2,1)S(1)}, f32[4,8,128]{2,1...) while((s32[]{:T(128)}, f32[4,8,512]{2,1,0:T(8,128)S(1)}, bf16[4,128,8,128]{3,1,2,0:T(8,128)(2,1)}, ...), condition=%wide.region_6.7_spmd, body=%wide.region_4.6_spmd.sunk | while | flops 136314880 | bytes 1385045 | solution.py:64
  40.4 1.7 %fusion.49 = f32[8,512]{1,0:T(8,128)S(1)} fusion(f32[8,128]{1,0:T(8,128)S(1)} %get-tuple-element.210, f32[8,128]{1,0:T(8,128)S(1)} %get-tuple-element.211, bf16[4,128,8,128]{3,1,2,0:T(8,128)(2,1)} %get-tuple-element.246, s32[]{:T(128)} %get-tuple-element.237, bf16[512,1024]{1,0:T(8,128)(2,1)S(1)} %get-tuple-element.247), kind=kOutput, calls=%fused_computation.20.clone.1 | convolution fusion | flops 136310784 | bytes 1335808 | tf_op jit(solution)/shard_map/while/body/eval_jaxpr/thd,nhd->htn/dot_general | solution.py:34
  42.1 1.7 %fusion.49 = f32[8,512]{1,0:T(8,128)S(1)} fusion(f32[8,128]{1,0:T(8,128)S(1)} %get-tuple-element.210, f32[8,128]{1,0:T(8,128)S(1)} %get-tuple-element.211, bf16[4,128,8,128]{3,1,2,0:T(8,128)(2,1)} %get-tuple-element.246, s32[]{:T(128)} %get-tuple-element.237, bf16[512,1024]{1,0:T(8,128)(2,1)S(1)} %get-tuple-element.247), kind=kOutput, calls=%fused_computation.20.clone.1 | convolution fusion | flops 136310784 | bytes 1335808 | tf_op jit(solution)/shard_map/while/body/eval_jaxpr/thd,nhd->htn/dot_general | solution.py:34
  43.9 1.7 %fusion.49 = f32[8,512]{1,0:T(8,128)S(1)} fusion(f32[8,128]{1,0:T(8,128)S(1)} %get-tuple-element.210, f32[8,128]{1,0:T(8,128)S(1)} %get-tuple-element.211, bf16[4,128,8,128]{3,1,2,0:T(8,128)(2,1)} %get-tuple-element.246, s32[]{:T(128)} %get-tuple-element.237, bf16[512,1024]{1,0:T(8,128)(2,1)S(1)} %get-tuple-element.247), kind=kOutput, calls=%fused_computation.20.clone.1 | convolution fusion | flops 136310784 | bytes 1335808 | tf_op jit(solution)/shard_map/while/body/eval_jaxpr/thd,nhd->htn/dot_general | solution.py:34
  45.6 1.7 %fusion.49 = f32[8,512]{1,0:T(8,128)S(1)} fusion(f32[8,128]{1,0:T(8,128)S(1)} %get-tuple-element.210, f32[8,128]{1,0:T(8,128)S(1)} %get-tuple-element.211, bf16[4,128,8,128]{3,1,2,0:T(8,128)(2,1)} %get-tuple-element.246, s32[]{:T(128)} %get-tuple-element.237, bf16[512,1024]{1,0:T(8,128)(2,1)S(1)} %get-tuple-element.247), kind=kOutput, calls=%fused_computation.20.clone.1 | convolution fusion | flops 136310784 | bytes 1335808 | tf_op jit(solution)/shard_map/while/body/eval_jaxpr/thd,nhd->htn/dot_general | solution.py:34
  47.3 0.0 copy-start.1
  47.4 16.3 %gather_fusion.3 = f32[2048]{0:T(1024)S(1)} fusion(f32[4,8,512]{2,1,0:T(8,128)S(1)} %get-tuple-element.60, s32[2048]{0:T(1024)S(1)} %reshape.253), kind=kCustom, calls=%fused_computation.3 | custom fusion | bytes 40960 | tf_op jit(solution)/shard_map/jit(take_along_axis)/gather | solution.py:83
  63.6 0.0 copy-done.1
  63.6 0.1 reshape.256
  63.7 0.0 all-to-all-done.1
  63.7 0.0 copy-start.3
  63.7 2.0 %gather_fusion.1 = bf16[256,1024]{1,0:T(8,128)(2,1)} fusion(bf16[512,1024]{1,0:T(8,128)(2,1)S(1)} %bitcast.98, s32[1024]{0:T(1024)S(1)} %pad_clamp_fusion), kind=kCustom, calls=%fused_computation.1 | custom fusion | bytes 1049600 | tf_op jit(solution)/shard_map/jit(_take)/gather | solution.py:81
  65.7 1.1 %copy.34 = bf16[32,8,8,128]{3,2,1,0:T(8,128)(2,1)S(1)} copy(bf16[32,8,8,128]{3,1,2,0:T(8,128)(2,1)} %bitcast.102) | data formatting | bytes 1048576
  66.8 0.0 copy-done.3
  66.8 0.7 %fusion.34 = f32[4,8,64]{2,1,0:T(8,128)S(1)} fusion(bf16[4,128,8,128]{1,3,2,0:T(8,128)(2,1)S(1)} %bitcast.101, bf16[4,64,8,128]{3,2,1,0:T(8,128)(2,1)S(1)} %bitcast.103, pred[4,64]{1,0:T(4,128)(4,1)S(1)} %compare_and_fusion.1), kind=kOutput, calls=%fused_computation.100 | convolution fusion | flops 68425856 | bytes 1581312 | tf_op jit(solution)/shard_map/div | solution.py:89
  67.6 0.7 reshape.230
  (45 shorter events, 0.5 us)
Async XLA Ops:
  0.6 19.4 %copy-start = (bf16[512,1024]{1,0:T(8,128)(2,1)S(1)}, bf16[512,1024]{1,0:T(8,128)(2,1)}, u32[]{:S(2)}) copy-start(bf16[512,1024]{1,0:T(8,128)(2,1)} %param.11) | copy-start | bytes 3145732
  0.6 3.8 %copy-start.6 = (s32[4,64]{1,0:T(4,128)S(1)}, s32[4,64]{1,0:T(4,128)}, u32[]{:S(2)}) copy-start(s32[4,64]{1,0:T(4,128)} %param.13) | copy-start | bytes 3076
  0.7 13.0 %copy-start.4 = (bf16[4,128,1024]{2,1,0:T(8,128)(2,1)S(1)}, bf16[4,128,1024]{2,1,0:T(8,128)(2,1)}, u32[]{:S(2)}) copy-start(bf16[4,128,1024]{2,1,0:T(8,128)(2,1)} %param.9) | copy-start | bytes 3145732
  0.7 19.3 %collective-permute-start = (bf16[128,1024]{1,0:T(8,128)(2,1)}, bf16[128,1024]{1,0:T(8,128)(2,1)S(1)}, u32[]{:S(2)}, u32[]{:S(2)}) collective-permute-start(bf16[128,1024]{1,0:T(8,128)(2,1)} %param.10), channel_id=1, source_target_pairs={{0,8},{8,16},{16,24},{24,0},{1,9},{9,17},{17,25},{25,1},{2,10},{10... | collective-permute-start | bytes 786440 | tf_op jit(solution)/shard_map/ppermute | solution.py:42
  6.5 13.4 %all-to-all-start = ((s32[8,1,64]{2,1,0:T(1,128)}), s32[8,1,64]{2,1,0:T(1,128)S(1)}, u32[]{:S(2)}, u32[]{:S(2)}) async-start(s32[8,1,64]{2,1,0:T(1,128)} %sub.64), calls=%async_computation | async-start | bytes 8192 | tf_op jit(solution)/shard_map/all_to_all | solution.py:76
  14.4 1.0 %copy-start.2 = (bf16[4,128,1024]{1,2,0:T(8,128)(2,1)}, bf16[4,128,1024]{1,2,0:T(8,128)(2,1)S(1)}, u32[]{:S(2)}) copy-start(bf16[4,128,1024]{1,2,0:T(8,128)(2,1)S(1)} %copy.26) | copy-start | bytes 3145732
  19.9 5.8 %collective-permute-start.1 = (bf16[128,1024]{1,0:T(8,128)(2,1)S(1)}, bf16[128,1024]{1,0:T(8,128)(2,1)S(1)}, u32[]{:S(2)}, u32[]{:S(2)}) collective-permute-start(bf16[128,1024]{1,0:T(8,128)(2,1)S(1)} %collective-permute-done), channel_id=1, source_target_pairs={{0,8},{8,16},{16,24},{24,0},{1,9},{9,17},{17,25},{25,1},{2,10},{10... | collective-permute-start | bytes 786440 | tf_op jit(solution)/shard_map/ppermute | solution.py:42
  25.7 5.8 %collective-permute-start.2 = (bf16[128,1024]{1,0:T(8,128)(2,1)S(1)}, bf16[128,1024]{1,0:T(8,128)(2,1)S(1)}, u32[]{:S(2)}, u32[]{:S(2)}) collective-permute-start(bf16[128,1024]{1,0:T(8,128)(2,1)S(1)} %collective-permute-done.1), channel_id=1, source_target_pairs={{0,8},{8,16},{16,24},{24,0},{1,9},{9,17},{17,25},{25,1},{2,10},{10... | collective-permute-start | bytes 786440 | tf_op jit(solution)/shard_map/ppermute | solution.py:42
  26.9 4.7 %copy-start.5 = (bf16[128,1024]{1,0:T(8,128)(2,1)S(1)}, bf16[128,1024]{1,0:T(8,128)(2,1)}, u32[]{:S(2)}) copy-start(bf16[128,1024]{1,0:T(8,128)(2,1)} %param.10) | copy-start | bytes 786436
  26.9 36.8 %all-to-all-start.1 = ((bf16[8,64,1024]{2,1,0:T(8,128)(2,1)}), bf16[8,64,1024]{2,1,0:T(8,128)(2,1)S(1)}, u32[]{:S(2)}, u32[]{:S(2)}) async-start(bf16[8,64,1024]{2,1,0:T(8,128)(2,1)} %broadcast_select_fusion), calls=%async_computation.1 | async-start | bytes 2097152 | tf_op jit(solution)/shard_map/all_to_all | solution.py:80
  47.3 16.3 %copy-start.1 = (f32[4,8,512]{2,1,0:T(8,128)}, f32[4,8,512]{2,1,0:T(8,128)S(1)}, u32[]{:S(2)}) copy-start(f32[4,8,512]{2,1,0:T(8,128)S(1)} %get-tuple-element.60) | copy-start | bytes 196612
  63.7 3.1 %copy-start.3 = (bf16[4,128,1024]{1,2,0:T(8,128)(2,1)S(1)}, bf16[4,128,1024]{1,2,0:T(8,128)(2,1)}, u32[]{:S(2)}) copy-start(bf16[4,128,1024]{1,2,0:T(8,128)(2,1)} %copy-done.2) | copy-start | bytes 3145732
